TPU v7x, 256 devices: a whole 4x4x8 slice. The times are simulated.
256 devices in a mesh: row: 16 (over y, x), col: 8 (over z), rep: 2 (over core).
Axes of the slice: x: 4, y: 4, z: 8, core: 2. Of those that a mesh axis runs over, the one named last changes fastest.
Arguments:
- patches: bfloat16 [2, 512, 6144], P('rep', 'col', 'row'), may hold values from -6 to 6
- cotangent: bfloat16 [2, 512, 6144], P('rep', 'col', 'row'), may hold values from -6 to 6
- w_in: bfloat16 [6144, 24576], P('row', 'col'), may hold values from -0.078125 to 0.078125
- w_out: bfloat16 [24576, 6144], P('col', 'row'), may hold values from -0.0390625 to 0.0390625
- moment_in: bfloat16 [2, 6144, 24576], P('rep', 'row', 'col'), may hold values from -2 to 2
- moment_out: bfloat16 [2, 24576, 6144], P('rep', 'col', 'row'), may hold values from -2 to 2
Outputs:
- mixed: bfloat16 [2, 512, 6144], P('rep', 'col', 'row')
- tally_in: bfloat16 [6144, 24576], P('row', 'col')
- tally_out: bfloat16 [24576, 6144], P('col', 'row')
All inputs are finite; a program needn't handle non-finite values.
Results may differ from a plain program's by a relative error of at most 0.0055.
Values may be sent and summed in bfloat16 or wider, within the bound.
A program may use at most 128 MiB of HBM per device.

v0:
```python
import math
import jax
import jax.numpy as jnp
from jax import lax
from jax.sharding import PartitionSpec as P

momentum_decay = 0.9
vote_scale = 0.3


def joined_along(blocks, dim):
    blocks = jnp.moveaxis(blocks, 0, dim)
    lengths = blocks.shape
    return blocks.reshape(*lengths[:dim], lengths[dim] * lengths[dim + 1], *lengths[dim + 2 :])


def sent_to_all(value, axis):
    copies = jnp.broadcast_to(value, (lax.axis_size(axis), *value.shape))
    return lax.all_to_all(copies, axis, split_axis=0, concat_axis=0, tiled=True)


def gather_directly(value, axis, dim):
    return joined_along(sent_to_all(value, axis), dim)


def cut_along(value, dim, peers):
    before, after = (value.shape[:dim], value.shape[dim + 1 :])
    return jnp.moveaxis(value.reshape(*before, peers, -1, *after), dim, 0)


def sum_at_owner(value, axis, dim):
    blocks = cut_along(value, dim, lax.axis_size(axis))
    arrived = lax.all_to_all(blocks, axis, split_axis=0, concat_axis=0, tiled=True)
    return arrived.sum(axis=0)


def gelu_value(pre):
    return 0.5 * pre * (1.0 + lax.erf(pre * (1.0 / math.sqrt(2.0))))


def gelu_slope(pre):
    return 0.5 * (1.0 + lax.erf(pre * (1.0 / math.sqrt(2.0)))) + pre * jnp.exp(-0.5 * pre * pre) * (
        1.0 / math.sqrt(2.0 * math.pi)
    )


def shards(patches, cotangent, w_in, w_out, moment_in, moment_out):
    inputs = gather_directly(patches[0], "col", 0)
    total_rows = inputs.shape[0]
    norm_factor = 1.0 / math.sqrt(total_rows)
    pre_whole = lax.psum(jnp.dot(inputs, w_in, preferred_element_type=jnp.float32), "row")
    hidden = gelu_value(pre_whole).astype(jnp.bfloat16)
    block = hidden
    mixed = sum_at_owner(
        jnp.dot(block, w_out, preferred_element_type=jnp.float32), "col", 0
    ).astype(jnp.bfloat16)
    grads = lax.all_gather(cotangent[0], "col", axis=0, tiled=True)
    block = grads
    back_whole = lax.psum(
        lax.dot_general(
            block, w_out, (((1,), (1,)), ((), ())), preferred_element_type=jnp.float32
        ).astype(jnp.bfloat16),
        "row",
    ).astype(jnp.float32)
    slope = (back_whole * gelu_slope(pre_whole)).astype(jnp.bfloat16)
    grad_first = (
        lax.dot_general(inputs, slope, (((0,), (0,)), ((), ())), preferred_element_type=jnp.float32)
        * norm_factor
    )
    grad_second = (
        lax.dot_general(hidden, grads, (((0,), (0,)), ((), ())), preferred_element_type=jnp.float32)
        * norm_factor
    )
    moved_first = (
        momentum_decay * moment_in[0].astype(jnp.float32) + (1.0 - momentum_decay) * grad_first
    )
    moved_second = (
        momentum_decay * moment_out[0].astype(jnp.float32) + (1.0 - momentum_decay) * grad_second
    )
    vote_first = jnp.tanh(moved_first / vote_scale).astype(jnp.bfloat16)
    vote_second = jnp.tanh(moved_second / vote_scale).astype(jnp.bfloat16)
    tally_first, tally_second = (
        lax.psum(vote_first, "rep").astype(jnp.float32),
        lax.psum(vote_second, "rep").astype(jnp.float32),
    )
    return (mixed[None], tally_first.astype(jnp.bfloat16), tally_second.astype(jnp.bfloat16))


def solution(mesh):
    in_specs = (
        P("rep", "col", "row"),
        P("rep", "col", "row"),
        P("row", "col"),
        P("col", "row"),
        P("rep", "row", "col"),
        P("rep", "col", "row"),
    )
    out_specs = (P("rep", "col", "row"), P("row", "col"), P("col", "row"))
    return jax.shard_map(shards, mesh=mesh, in_specs=in_specs, out_specs=out_specs, check_vma=False)
```

profile of v0, /device:TPU:1, one launch (start us, length us, event | category | flops | bytes accessed | tf_op | source)
XLA Modules:
  0.0 338.2 jit_solution(2649844550422343762)
XLA Ops:
  7.2 0.0 copy-start
  7.2 0.0 all-reduce.5.cloned.1.call-start
  7.2 1.0 broadcast_in_dim.4
  8.2 22.4 %all_to_all.10 = bf16[8,64,384]{2,1,0:T(8,128)(2,1)S(1)} all-to-all(bf16[8,64,384]{2,1,0:T(8,128)(2,1)S(1)} %broadcast_in_dim.4), channel_id=1, replica_groups=mesh['row'=16,'col'=8,'rep'=2] {'col'}, dimensions={0} | all-to-all | bytes 786432 | tf_op jit(solution)/shard_map/all_to_all | solution.py:19
  30.6 6.1 %fusion.20 = f32[512,3072]{1,0:T(8,128)} fusion(bf16[512,384]{1,0:T(8,128)(2,1)S(1)} %bitcast.36, bf16[384,3072]{1,0:T(8,128)(2,1)} %param.8), kind=kOutput, calls=%fused_computation.26 | convolution fusion | flops 1207959552 | bytes 9043968 | tf_op jit(solution)/shard_map/dot_general | solution.py:51
  36.7 0.0 copy-start.2
  36.7 0.0 all-reduce.5.cloned.1.call-update
  36.7 0.0 all-reduce.7.cloned.1.call-start
  36.8 0.7 copy-done.2
  37.5 20.5 %all-gather = bf16[1,512,384]{2,1,0:T(8,128)(2,1)S(1)} all-gather(bf16[1,64,384]{2,1,0:T(8,128)(2,1)S(1)} %copy-done.2), channel_id=2, replica_groups=mesh['row'=16,'col'=8,'rep'=2] {'col'}, dimensions={1}, use_global_device_ids=true | all-gather | bytes 442368 | tf_op jit(solution)/shard_map/all_gather | solution.py:57
  58.0 0.0 copy-done
  58.0 3.5 %convolution_convert_fusion = bf16[512,3072]{1,0:T(8,128)(2,1)} fusion(bf16[3072,384]{1,0:T(8,128)(2,1)S(1)} %copy-done, bf16[1,512,384]{2,1,0:T(8,128)(2,1)S(1)} %all-gather), kind=kOutput, calls=%fused_computation.17 | convolution fusion | flops 1209532416 | bytes 5898240 | tf_op jit(solution)/shard_map/dot_general | solution.py:60
  61.4 0.0 all-reduce.7.cloned.1.call-update
  61.5 0.0 all-reduce.9.cloned.1.call-start
  61.5 4.3 %copy.9 = bf16[1,384,3072]{1,2,0:T(8,128)(2,1)} copy(bf16[1,384,3072]{2,1,0:T(8,128)(2,1)} %param.10) | data formatting | bytes 4718592 | tf_op args[4]
  65.8 101.0 %all-reduce.5.cloned.1.call-done = f32[512,3072]{1,0:T(8,128)} async-done(((f32[512,3072]{1,0:T(8,128)}), f32[512,3072]{1,0:T(8,128)}) %all-reduce.5.cloned.1.call-update) | async-done | bytes 6291472 | tf_op jit(solution)/shard_map/psum | solution.py:51
  166.8 0.0 copy-start.3
  166.8 3.6 %multiply_convert_fusion = bf16[512,3072]{1,0:T(8,128)(2,1)S(1)} fusion(f32[512,3072]{1,0:T(8,128)} %all-reduce.5.cloned.1.call-done), kind=kLoop, calls=%fused_computation.7 | loop fusion | flops 7864320 | bytes 9437184 | tf_op jit(solution)/shard_map/convert_element_type | solution.py:52
  170.4 0.0 copy-start.1
  170.4 1.7 copy-done.1
  172.1 0.0 copy-done.3
  172.1 4.0 %fusion.8 = bf16[3072,384]{1,0:T(8,128)(2,1)} fusion(bf16[1,3072,384]{2,1,0:T(8,128)(2,1)S(1)} %copy-done.3, bf16[512,3072]{1,0:T(8,128)(2,1)S(1)} %multiply_convert_fusion, bf16[1,512,384]{2,1,0:T(8,128)(2,1)S(1)} %all-gather), kind=kOutput, calls=%fused_computation.12 | convolution fusion | flops 1215037440 | bytes 8257536 | tf_op jit(solution)/shard_map/dot_general | solution.py:71
  176.1 99.6 %all-reduce.7.cloned.1.call-done = bf16[512,3072]{1,0:T(8,128)(2,1)} async-done(((bf16[512,3072]{1,0:T(8,128)(2,1)}), bf16[512,3072]{1,0:T(8,128)(2,1)}) %all-reduce.7.cloned.1.call-update) | async-done | bytes 3145744 | tf_op jit(solution)/shard_map/psum | solution.py:59
  275.7 8.4 %fusion.11 = bf16[384,3072]{0,1:T(8,128)(2,1)} fusion(bf16[1,384,3072]{1,2,0:T(8,128)(2,1)} %copy.9, bf16[512,384]{1,0:T(8,128)(2,1)S(1)} %bitcast.37, f32[512,3072]{1,0:T(8,128)} %all-reduce.5.cloned.1.call-done, bf16[512,3072]{1,0:T(8,128)(2,1)} %all-reduce.7.cloned.1.call-done), kind=kOutput, calls=%fused_computation.16 | convolution fusion | flops 1232338944 | bytes 14548992 | tf_op jit(solution)/shard_map/dot_general | solution.py:67
  284.1 0.0 all-reduce.9.cloned.1.call-update
  284.1 3.7 %fusion.21 = f32[512,384]{1,0:T(8,128)S(1)} fusion(bf16[512,3072]{1,0:T(8,128)(2,1)} %copy-done.1, bf16[3072,384]{1,0:T(8,128)(2,1)S(1)} %copy-done), kind=kOutput, calls=%fused_computation.27 | convolution fusion | flops 1207959552 | bytes 6291456 | tf_op jit(solution)/shard_map/dot_general | solution.py:55
  287.8 27.9 %all_to_all.11 = f32[8,64,384]{2,1,0:T(8,128)S(1)} all-to-all(f32[8,64,384]{2,1,0:T(8,128)S(1)} %bitcast.38), channel_id=1, replica_groups=mesh['row'=16,'col'=8,'rep'=2] {'col'}, dimensions={0} | all-to-all | bytes 1572864 | tf_op jit(solution)/shard_map/all_to_all | solution.py:33
  315.7 0.7 reduce_sum.9
  316.4 7.7 %all-reduce.9.cloned.1.call-done = (bf16[384,3072]{0,1:T(8,128)(2,1)}, bf16[3072,384]{1,0:T(8,128)(2,1)}) async-done(((bf16[384,3072]{0,1:T(8,128)(2,1)}, bf16[3072,384]{1,0:T(8,128)(2,1)}), (bf16[384,3072]{0,1:T(8,128)(2,1)}, bf16[3072,384]{1,0:T(8,128)(2,1)})) %all-reduce.9.cloned.1.call-update) | async-done | bytes 4718608 | tf_op jit(solution)/shard_map/psum | solution.py:83
  324.1 4.3 %copy.10 = bf16[384,3072]{1,0:T(8,128)(2,1)} copy(bf16[384,3072]{0,1:T(8,128)(2,1)} %get-tuple-element.6) | data formatting | bytes 4718592
  328.4 3.3 copy.15
Async XLA Ops:
  7.2 50.8 %copy-start = (bf16[3072,384]{1,0:T(8,128)(2,1)S(1)}, bf16[3072,384]{1,0:T(8,128)(2,1)}, u32[]{:S(2)}) copy-start(bf16[3072,384]{1,0:T(8,128)(2,1)} %param.9) | copy-start | bytes 7077892
  7.2 159.7 %all-reduce.5.cloned.1.call-start = ((), (), s32[]{:S(2)}) async-start(), calls=%async_computation.2 | async-start | bytes 12582912 | tf_op jit(solution)/shard_map/psum | solution.py:51
  36.7 0.8 copy-start.2
  36.7 239.0 %all-reduce.7.cloned.1.call-start = ((), (), s32[]{:S(2)}) async-start(), calls=%async_computation.3 | async-start | bytes 6291456 | tf_op jit(solution)/shard_map/psum | solution.py:59
  61.5 262.7 %all-reduce.9.cloned.1.call-start = ((), (), s32[]{:S(2)}) async-start(), calls=%async_computation.4 | async-start | bytes 9437184 | tf_op jit(solution)/shard_map/psum | solution.py:83
  166.8 5.3 %copy-start.3 = (bf16[1,3072,384]{2,1,0:T(8,128)(2,1)S(1)}, bf16[1,3072,384]{2,1,0:T(8,128)(2,1)}, u32[]{:S(2)}) copy-start(bf16[1,3072,384]{2,1,0:T(8,128)(2,1)} %param.11) | copy-start | bytes 7077892
  170.4 1.7 copy-start.1
Sparse Core Ops, SparseCore 0:
  36.9 129.9 all-reduce.4
  170.2 105.4 all-reduce.6
  284.2 39.8 all-reduce.8
where the time goes:
time: 339 us; the launch traced here: 338 us
  waiting for transfers between devices  208 us (61%)
  blocking collectives  70.8 us (21%)
  matrix products  25.6 us (8%)
  local copies, waits for them, and re-layouts  15.3 us (5%)
  between operations  13.8 us (4%)
  other arithmetic  4.23 us (1%)
    psum x1, waiting for transfers between devices, shards(): lax.psum(jnp.dot(inputs, w_in, preferred_element_type=jnp.float32), 'row')  101 us
    psum x1, waiting for transfers between devices, shards(): lax.psum(lax.dot_general(block, w_out, (((1,), (1,)), ((), ())), preferre...  99.6 us
    all_to_all x1, blocking collectives, sum_at_owner(): lax.all_to_all(blocks, axis, split_axis=0, concat_axis=0, tiled=True)  27.9 us
    all_to_all x1, blocking collectives, sent_to_all(): return lax.all_to_all(copies, axis, split_axis=0, concat_axis=0, tiled=True)  22.4 us
    all_gather x1, blocking collectives, shards(): grads = lax.all_gather(cotangent[0], 'col', axis=0, tiled=True)  20.5 us
    unnamed x11, local copies, waits for them, and re-layouts  14.3 us
    dot_general x1, matrix products, shards(): lax.dot_general(inputs, slope, (((0,), (0,)), ((), ())), preferred_elemen...  8.39 us
    psum x1, waiting for transfers between devices, shards(): lax.psum(vote_first, 'rep').astype(jnp.float32)  7.74 us
  transfers between devices with their start and end apart: 3, of which 3 were waited for; matrix products, arithmetic and copies ran while one was open for 6% of the time, Pallas kernels for 0%

commit v1 on v0

--- a/solution.py
+++ b/solution.py
@@ -6,6 +6,11 @@
 
 momentum_decay = 0.9
 vote_scale = 0.3
+
+
+def gather_from_all(value, axis, dim):
+    copies = jnp.concatenate([value] * lax.axis_size(axis), axis=dim)
+    return lax.all_to_all(copies, axis, dim, dim, tiled=True)
 
 
 def joined_along(blocks, dim):
@@ -54,7 +59,7 @@
     mixed = sum_at_owner(
         jnp.dot(block, w_out, preferred_element_type=jnp.float32), "col", 0
     ).astype(jnp.bfloat16)
-    grads = lax.all_gather(cotangent[0], "col", axis=0, tiled=True)
+    grads = gather_from_all(cotangent[0], "col", 0)
     block = grads
     back_whole = lax.psum(
         lax.dot_general(

time: 339 us -> 339 us (level)
  waiting for transfers between devices: 208 us -> 215 us
  blocking collectives: 70.8 us -> 64.4 us
    all_gather x1 -> x0, blocking collectives: 20.5 us -> none  [shards(): grads = lax.all_gather(cotangent[0], 'col', axis=0, tiled=True)]
    all_to_all x0 -> x1, blocking collectives: none -> 14.1 us  [gather_from_all(): return lax.all_to_all(copies, axis, dim, dim, tiled=True)]
    psum x1, waiting for transfers between devices: 101 us -> 107 us  [shards(): lax.psum(jnp.dot(inputs, w_in, preferred_element_type=jnp.float32), 'row')]
    unnamed x11 -> x18, local copies, waits for them, and re-layouts: 14.3 us -> 14.4 us
where the time goes in v1:
time: 339 us; the launch traced here: 338 us
  waiting for transfers between devices  215 us (63%)
  blocking collectives  64.4 us (19%)
  matrix products  25.6 us (8%)
  local copies, waits for them, and re-layouts  15.4 us (5%)
  between operations  13.8 us (4%)
  other arithmetic  4.23 us (1%)
    psum x1, waiting for transfers between devices, shards(): lax.psum(jnp.dot(inputs, w_in, preferred_element_type=jnp.float32), 'row')  107 us
    psum x1, waiting for transfers between devices, shards(): lax.psum(lax.dot_general(block, w_out, (((1,), (1,)), ((), ())), preferre...  99.6 us
    all_to_all x1, blocking collectives, sum_at_owner(): lax.all_to_all(blocks, axis, split_axis=0, concat_axis=0, tiled=True)  27.9 us
    all_to_all x1, blocking collectives, sent_to_all(): return lax.all_to_all(copies, axis, split_axis=0, concat_axis=0, tiled=True)  22.4 us
    unnamed x18, local copies, waits for them, and re-layouts  14.4 us
    all_to_all x1, blocking collectives, gather_from_all(): return lax.all_to_all(copies, axis, dim, dim, tiled=True)  14.1 us
    dot_general x1, matrix products, shards(): lax.dot_general(inputs, slope, (((0,), (0,)), ((), ())), preferred_elemen...  8.39 us
    psum x1, waiting for transfers between devices, shards(): lax.psum(vote_first, 'rep').astype(jnp.float32)  7.74 us
  transfers between devices with their start and end apart: 3, of which 3 were waited for; matrix products, arithmetic and copies ran while one was open for 6% of the time, Pallas kernels for 0%

profile of v1, /device:TPU:1, one launch (start us, length us, event | category | flops | bytes accessed | tf_op | source)
XLA Modules:
  0.0 338.2 jit_solution(2819725202058421522)
XLA Ops:
  7.2 0.0 copy-start
  7.2 0.0 all-reduce.5.cloned.1.call-start
  7.2 1.0 broadcast_in_dim.4
  8.2 22.4 %all_to_all.22 = bf16[8,64,384]{2,1,0:T(8,128)(2,1)S(1)} all-to-all(bf16[8,64,384]{2,1,0:T(8,128)(2,1)S(1)} %broadcast_in_dim.4), channel_id=1, replica_groups=mesh['row'=16,'col'=8,'rep'=2] {'col'}, dimensions={0} | all-to-all | bytes 786432 | tf_op jit(solution)/shard_map/all_to_all | solution.py:24
  30.6 6.1 %fusion.18 = f32[512,3072]{1,0:T(8,128)} fusion(bf16[512,384]{1,0:T(8,128)(2,1)S(1)} %bitcast.44, bf16[384,3072]{1,0:T(8,128)(2,1)} %param.8), kind=kOutput, calls=%fused_computation.32 | convolution fusion | flops 1207959552 | bytes 9043968 | tf_op jit(solution)/shard_map/dot_general | solution.py:56
  36.7 0.0 copy-start.1
  36.7 0.0 all-reduce.5.cloned.1.call-update
  36.7 0.0 all-reduce.7.cloned.1.call-start
  36.8 0.7 copy-done.1
  37.6 14.1 %all_to_all.23 = bf16[8,64,384]{2,1,0:T(8,128)(2,1)S(1)} all-to-all(bf16[8,64,384]{2,1,0:T(8,128)(2,1)S(1)} %bitcast.47), channel_id=1, replica_groups=mesh['row'=16,'col'=8,'rep'=2] {'col'}, dimensions={0} | all-to-all | bytes 786432 | tf_op jit(solution)/shard_map/all_to_all | solution.py:13
  51.8 0.0 copy-done
  51.8 3.5 %convolution_convert_fusion = bf16[512,3072]{1,0:T(8,128)(2,1)} fusion(bf16[512,384]{1,0:T(8,128)(2,1)S(1)} %bitcast.48, bf16[3072,384]{1,0:T(8,128)(2,1)S(1)} %copy-done), kind=kOutput, calls=%fused_computation.17 | convolution fusion | flops 1209532416 | bytes 5898240 | tf_op jit(solution)/shard_map/dot_general | solution.py:65
  55.2 0.0 all-reduce.7.cloned.1.call-update
  55.3 0.0 all-reduce.9.cloned.1.call-start
  55.3 4.3 %copy.9 = bf16[1,384,3072]{1,2,0:T(8,128)(2,1)} copy(bf16[1,384,3072]{2,1,0:T(8,128)(2,1)} %param.10) | data formatting | bytes 4718592 | tf_op args[4]
  59.6 107.2 %all-reduce.5.cloned.1.call-done = f32[512,3072]{1,0:T(8,128)} async-done(((f32[512,3072]{1,0:T(8,128)}), f32[512,3072]{1,0:T(8,128)}) %all-reduce.5.cloned.1.call-update) | async-done | bytes 6291472 | tf_op jit(solution)/shard_map/psum | solution.py:56
  166.8 0.0 copy-start.3
  166.8 3.6 %multiply_convert_fusion = bf16[512,3072]{1,0:T(8,128)(2,1)S(1)} fusion(f32[512,3072]{1,0:T(8,128)} %all-reduce.5.cloned.1.call-done), kind=kLoop, calls=%fused_computation.7 | loop fusion | flops 7864320 | bytes 9437184 | tf_op jit(solution)/shard_map/convert_element_type | solution.py:57
  170.4 0.0 copy-start.2
  170.4 1.7 copy-done.2
  172.1 0.0 copy-done.3
  172.1 4.0 %fusion.8 = bf16[3072,384]{1,0:T(8,128)(2,1)} fusion(bf16[1,3072,384]{2,1,0:T(8,128)(2,1)S(1)} %copy-done.3, bf16[512,3072]{1,0:T(8,128)(2,1)S(1)} %multiply_convert_fusion, bf16[512,384]{1,0:T(8,128)(2,1)S(1)} %bitcast.49), kind=kOutput, calls=%fused_computation.12 | convolution fusion | flops 1215037440 | bytes 8257536 | tf_op jit(solution)/shard_map/dot_general | solution.py:76
  176.1 99.6 %all-reduce.7.cloned.1.call-done = bf16[512,3072]{1,0:T(8,128)(2,1)} async-done(((bf16[512,3072]{1,0:T(8,128)(2,1)}), bf16[512,3072]{1,0:T(8,128)(2,1)}) %all-reduce.7.cloned.1.call-update) | async-done | bytes 3145744 | tf_op jit(solution)/shard_map/psum | solution.py:64
  275.7 8.4 %fusion.11 = bf16[384,3072]{0,1:T(8,128)(2,1)} fusion(bf16[1,384,3072]{1,2,0:T(8,128)(2,1)} %copy.9, bf16[512,384]{1,0:T(8,128)(2,1)S(1)} %bitcast.45, f32[512,3072]{1,0:T(8,128)} %all-reduce.5.cloned.1.call-done, bf16[512,3072]{1,0:T(8,128)(2,1)} %all-reduce.7.cloned.1.call-done), kind=kOutput, calls=%fused_computation.16 | convolution fusion | flops 1232338944 | bytes 14548992 | tf_op jit(solution)/shard_map/dot_general | solution.py:72
  284.1 0.0 all-reduce.9.cloned.1.call-update
  284.1 3.7 %fusion.19 = f32[512,384]{1,0:T(8,128)S(1)} fusion(bf16[512,3072]{1,0:T(8,128)(2,1)} %copy-done.2, bf16[3072,384]{1,0:T(8,128)(2,1)S(1)} %copy-done), kind=kOutput, calls=%fused_computation.33 | convolution fusion | flops 1207959552 | bytes 6291456 | tf_op jit(solution)/shard_map/dot_general | solution.py:60
  287.8 27.9 %all_to_all.24 = f32[8,64,384]{2,1,0:T(8,128)S(1)} all-to-all(f32[8,64,384]{2,1,0:T(8,128)S(1)} %bitcast.46), channel_id=1, replica_groups=mesh['row'=16,'col'=8,'rep'=2] {'col'}, dimensions={0} | all-to-all | bytes 1572864 | tf_op jit(solution)/shard_map/all_to_all | solution.py:38
  315.7 0.7 reduce_sum.9
  316.4 7.7 %all-reduce.9.cloned.1.call-done = (bf16[384,3072]{0,1:T(8,128)(2,1)}, bf16[3072,384]{1,0:T(8,128)(2,1)}) async-done(((bf16[384,3072]{0,1:T(8,128)(2,1)}, bf16[3072,384]{1,0:T(8,128)(2,1)}), (bf16[384,3072]{0,1:T(8,128)(2,1)}, bf16[3072,384]{1,0:T(8,128)(2,1)})) %all-reduce.9.cloned.1.call-update) | async-done | bytes 4718608 | tf_op jit(solution)/shard_map/psum | solution.py:88
  324.1 4.3 %copy.10 = bf16[384,3072]{1,0:T(8,128)(2,1)} copy(bf16[384,3072]{0,1:T(8,128)(2,1)} %get-tuple-element.6) | data formatting | bytes 4718592
  328.4 3.3 copy.22
  (8 shorter events, 0.1 us)
Async XLA Ops:
  7.2 44.6 %copy-start = (bf16[3072,384]{1,0:T(8,128)(2,1)S(1)}, bf16[3072,384]{1,0:T(8,128)(2,1)}, u32[]{:S(2)}) copy-start(bf16[3072,384]{1,0:T(8,128)(2,1)} %param.9) | copy-start | bytes 7077892
  7.2 159.7 %all-reduce.5.cloned.1.call-start = ((), (), s32[]{:S(2)}) async-start(), calls=%async_computation.3 | async-start | bytes 12582912 | tf_op jit(solution)/shard_map/psum | solution.py:56
  36.7 0.8 copy-start.1
  36.7 239.0 %all-reduce.7.cloned.1.call-start = ((), (), s32[]{:S(2)}) async-start(), calls=%async_computation.4 | async-start | bytes 6291456 | tf_op jit(solution)/shard_map/psum | solution.py:64
  55.3 268.9 %all-reduce.9.cloned.1.call-start = ((), (), s32[]{:S(2)}) async-start(), calls=%async_computation.5 | async-start | bytes 9437184 | tf_op jit(solution)/shard_map/psum | solution.py:88
  166.8 5.3 %copy-start.3 = (bf16[1,3072,384]{2,1,0:T(8,128)(2,1)S(1)}, bf16[1,3072,384]{2,1,0:T(8,128)(2,1)}, u32[]{:S(2)}) copy-start(bf16[1,3072,384]{2,1,0:T(8,128)(2,1)} %param.11) | copy-start | bytes 7077892
  170.4 1.7 copy-start.2
Sparse Core Ops, SparseCore 0:
  36.9 129.9 all-reduce.4
  170.2 105.4 all-reduce.6
  284.2 39.8 all-reduce.8
